TPU v7x, 128 devices: a whole 4x4x4 slice. The times are simulated.
128 devices in a mesh: grp: 32 (over x, z, y_lo), sub: 4 (over y_hi, core).
Axes of the slice: x: 4, y: 4 (y_hi: 2, y_lo: 2; y = y_hi * 2 + y_lo), z: 4, core: 2. Of those that a mesh axis runs over, the one named last changes fastest.
Arguments:
- gate_source: bfloat16 [128, 2048, 768], P('grp', 'sub'), may hold values from -0.125 to 0.125
- up_source: bfloat16 [128, 2048, 768], P('grp', 'sub'), may hold values from -0.125 to 0.125
- down_source: bfloat16 [128, 2048, 768], P('grp', 'sub'), may hold values from -0.21875 to 0.21875
- source_order: int32 [128], replicated, may hold values from 0 to 127, each once
- target_order: int32 [128], replicated, may hold values from 0 to 127, each once
Outputs:
- packed: bfloat16 [3, 32, 4, 8, 96, 2048], P(None, 'grp', 'sub')
- scales: float32 [3, 32, 4, 16, 768], P(None, 'grp', 'sub')
Inputs may be any that keep to these rules, and one draw needn't show every extreme that they name: `source_order`: each expert number appears once. `target_order`: each expert number appears once.
All inputs are finite; a program needn't handle non-finite values. Where the computation divides by a largest or mean magnitude, that divisor is 1e-20 or more.
Results may differ from a plain program's by a relative error of at most 0.001.
Values may be sent and summed in bfloat16 or wider, within the bound.
A program may use at most 192 MiB of HBM per device.

v0:
```python
import jax
import jax.numpy as jnp
from jax import lax
from jax.sharding import PartitionSpec as P

BLOCK = 128


EPS = 1e-06


def per_device(gate_source, up_source, down_source, source_order, target_order):
    stacked = jnp.stack([gate_source, up_source, down_source])
    matrices, local_slots, local_rows, hidden = stacked.shape
    groups = lax.axis_size("grp")
    shards = lax.axis_size("sub")
    devices = groups * shards
    experts = local_slots * groups
    full_rows = local_rows * shards
    targets = groups // 2
    per_group = experts // targets
    splits = 2 * shards
    columns = hidden // splits
    matches = (source_order[None, :] == target_order[:, None]).astype(jnp.int32)
    picked = jnp.sum(matches * jnp.arange(experts, dtype=jnp.int32)[None, :], axis=1)
    slab_rows = local_rows // devices
    pieces = stacked.reshape(matrices, 1, local_slots, devices, slab_rows, hidden)
    received = lax.all_to_all(pieces, ("grp", "sub"), split_axis=3, concat_axis=1, tiled=True)
    received = received.reshape(matrices, groups, shards, local_slots, slab_rows, hidden)
    received = received.transpose(0, 1, 3, 2, 4, 5).reshape(
        matrices, experts, shards * slab_rows, hidden
    )
    ordered = jnp.take(received, picked, axis=1)
    outgoing = ordered.reshape(matrices, targets, per_group, shards * slab_rows, splits, columns)
    outgoing = outgoing.transpose(0, 1, 4, 2, 3, 5).reshape(
        matrices, devices, per_group, 1, shards * slab_rows, columns
    )
    placed = lax.all_to_all(outgoing, ("grp", "sub"), split_axis=1, concat_axis=3, tiled=True)
    placed = placed.reshape(matrices, per_group, devices, shards, slab_rows, columns)
    placed = placed.transpose(0, 1, 3, 2, 4, 5).reshape(matrices, per_group, full_rows, columns)
    num_blocks = full_rows // BLOCK
    blocks = placed.astype(jnp.float32).reshape(matrices, per_group, num_blocks, BLOCK, columns)
    block_scale = jnp.max(jnp.abs(blocks), axis=3) + EPS
    quantized = (blocks / block_scale[:, :, :, None, :]).astype(jnp.bfloat16)
    quantized = quantized.reshape(matrices, per_group, full_rows, columns).transpose(0, 1, 3, 2)
    quantized = quantized.reshape(matrices, 1, 1, per_group, columns, full_rows)
    block_scale = block_scale.transpose(0, 2, 1, 3).reshape(
        matrices, 1, 1, num_blocks, per_group * columns
    )
    return (quantized, block_scale)


def solution(mesh):
    placed = (P("grp", "sub", None), P("grp", "sub", None), P("grp", "sub", None), P(), P())
    return jax.shard_map(
        per_device,
        mesh=mesh,
        in_specs=placed,
        out_specs=(P(None, "grp", "sub", None, None, None), P(None, "grp", "sub", None, None)),
        check_vma=False,
    )
```

profile of v0, /device:TPU:1, one launch (start us, length us, event | category | flops | bytes accessed | tf_op | source)
XLA Modules:
  0.0 516.9 jit_solution(9932338294605098806)
XLA Ops:
  0.6 4.5 copy.46
  5.1 4.3 copy.47
  9.4 2.4 copy.48
  11.9 8.1 %pad_maximum_fusion = bf16[3,1,4,128,4,768]{5,2,4,3,1,0:T(4,128)(2,1)S(1)} fusion(bf16[1,1,4,128,4,768]{5,2,4,3,1,0:T(4,128)(2,1)S(1)} %bitcast.58, bf16[1,1,4,128,4,768]{5,2,4,3,1,0:T(4,128)(2,1)S(1)} %bitcast.57, bf16[1,1,4,128,4,768]{5,2,4,3,1,0:T(4,128)(2,1)S(1)} %bitcast.56), kind=kLoop, calls=%fused_computation.4 | loop fusion | flops 9437184 | bytes 18874368 | tf_op jit(solution)/shard_map/stack | solution.py:13
  20.0 4.5 copy.49
  24.5 11.9 %all-to-all-start = ((bf16[3,1,4,128,4,768]{5,4,2,0,1,3:T(4,128)(2,1)}), bf16[3,1,4,128,4,768]{5,4,2,0,1,3:T(4,128)(2,1)}, u32[]{:S(2)}, u32[]{:S(2)}) async-start(bf16[3,1,4,128,4,768]{5,4,2,0,1,3:T(4,128)(2,1)} %copy.49), calls=%async_computation | async-start | bytes 18874368 | tf_op jit(solution)/shard_map/all_to_all | solution.py:28
  36.7 121.2 %all-to-all-done = bf16[3,1,4,128,4,768]{5,4,2,0,1,3:T(4,128)(2,1)} async-done(((bf16[3,1,4,128,4,768]{5,4,2,0,1,3:T(4,128)(2,1)}), bf16[3,1,4,128,4,768]{5,4,2,0,1,3:T(4,128)(2,1)}, u32[]{:S(2)}, u32[]{:S(2)}) %all-to-all-start) | async-done | bytes 9437216 | tf_op jit(solution)/shard_map/all_to_all | solution.py:28
  157.9 9.0 %copy.51 = bf16[3,32,4,4,4,768]{5,4,3,2,1,0:T(4,128)(2,1)} copy(bf16[3,32,4,4,4,768]{5,4,2,0,3,1:T(4,128)(2,1)} %bitcast.7) | data formatting | bytes 18874368 | tf_op jit(solution)/shard_map/transpose | solution.py:30
  166.9 15.6 %reshape.70 = bf16[3,128,16,768]{3,2,1,0:T(8,128)(2,1)} reshape(bf16[3,32,4,4,4,768]{5,4,3,2,1,0:T(4,128)(2,1)} %copy.51) | data formatting | bytes 18874368 | tf_op jit(solution)/shard_map/reshape | solution.py:30
  182.4 11.0 %gather_fusion = bf16[128,3,16,768]{3,2,1,0:T(8,128)(2,1)} fusion(bf16[3,128,16,768]{3,2,1,0:T(8,128)(2,1)} %reshape.70, s32[1024]{0:T(1024)S(1)} %pad_clamp_fusion), kind=kCustom, calls=%fused_computation | custom fusion | bytes 18874880 | tf_op jit(solution)/shard_map/jit(_take)/gather | solution.py:33
  193.4 21.7 %gather.7 = bf16[3,16,8,16,8,96]{5,4,3,0,2,1:T(8,128)(2,1)} reshape(bf16[3,128,16,768]{3,2,0,1:T(8,128)(2,1)} %bitcast.53) | data formatting | bytes 18874368 | tf_op jit(solution)/shard_map/jit(_take)/gather | solution.py:33
  215.2 7.7 %copy_select_fusion = bf16[3,16,8,16,8,96]{5,3,2,4,1,0:T(8,128)(2,1)S(1)} fusion(bf16[3,16,8,16,8,96]{5,4,3,0,2,1:T(8,128)(2,1)} %gather.7, pred[16,8]{1,0:T(8,128)(4,1)S(1)} %compare_and_fusion), kind=kLoop, calls=%fused_computation.2 | loop fusion | flops 4718592 | bytes 18874496 | tf_op jit(solution)/shard_map/jit(_take)/select_n | solution.py:33
  224.6 148.8 %all_to_all.27 = bf16[3,128,8,1,16,96]{5,4,2,0,3,1:T(8,128)(2,1)} all-to-all(bf16[3,128,8,1,16,96]{5,4,2,0,3,1:T(8,128)(2,1)S(1)} %copy.53), channel_id=1, replica_groups=mesh['grp'=32,'sub'=4] {'grp','sub'}, dimensions={1} | all-to-all | bytes 18874368 | tf_op jit(solution)/shard_map/all_to_all | solution.py:38
  373.4 15.7 %copy.54 = bf16[3,128,8,1,16,96]{1,5,4,2,0,3:T(8,128)(2,1)} copy(bf16[3,128,8,1,16,96]{5,4,2,0,3,1:T(8,128)(2,1)} %all_to_all.27) | data formatting | bytes 18874368 | tf_op jit(solution)/shard_map/all_to_all | solution.py:38
  389.1 12.9 %fusion.1 = f32[3,128,1,8,1,16,96]{1,6,5,4,3,2,0:T(8,128)} fusion(bf16[3,128,8,1,16,96]{1,5,4,2,0,3:T(8,128)(2,1)} %copy.54), kind=kLoop, calls=%fused_computation.6 | loop fusion | flops 9437184 | bytes 28311552 | tf_op jit(solution)/shard_map/abs | solution.py:43
  402.0 12.8 %bitcast_convert_fusion = f32[3,128,1,8,1,16,96]{1,6,5,4,3,2,0:T(8,128)} fusion(bf16[3,128,8,1,16,96]{1,5,4,2,0,3:T(8,128)(2,1)} %copy.54), kind=kLoop, calls=%fused_computation.5 | loop fusion | flops 4718592 | bytes 28311552 | tf_op jit(solution)/shard_map/convert_element_type | solution.py:42
  414.8 11.7 %reduce_max.11 = f32[3,8,128,4,96]{2,4,3,1,0:T(8,128)} reduce(f32[3,8,128,4,4,96]{2,5,4,3,1,0:T(8,128)} %bitcast.50, f32[]{:T(128)} %constant.20.clone.1), dimensions={4}, to_apply=%region_1.2 | reduce | flops 3538944 | bytes 23592964 | tf_op jit(solution)/shard_map/reduce_max | solution.py:43
  426.5 7.2 %copy.63 = f32[3,8,128,4,96]{4,3,1,2,0:T(4,128)} copy(f32[3,8,128,4,96]{2,4,3,1,0:T(8,128)} %reduce_max.11) | data formatting | bytes 9437184
  433.7 9.1 %copy.57 = f32[3,8,4,128,96]{4,3,2,1,0:T(8,128)} copy(f32[3,8,4,128,96]{4,2,1,3,0:T(4,128)} %bitcast.55) | data formatting | bytes 9437184 | tf_op jit(solution)/shard_map/reduce_max | solution.py:43
  442.7 4.3 reduce_max.21
  448.0 22.3 %copy.55 = f32[3,8,4,128,4,96]{5,1,4,3,2,0:T(8,128)} copy(f32[3,8,4,128,4,96]{3,5,4,2,1,0:T(8,128)} %bitcast.51) | data formatting | bytes 37748736 | tf_op jit(solution)/shard_map/convert_element_type | solution.py:42
  470.3 9.9 %div.11 = f32[3,8,16,128,96]{4,1,3,2,0:T(8,128)} broadcast(f32[3,8,16,96]{3,1,2,0:T(8,128)S(1)} %copy.58), dimensions={0,1,2,4} | broadcast | bytes 19021824 | tf_op jit(solution)/shard_map/div | solution.py:44
  480.2 21.2 %fusion = bf16[3,1,1,8,96,2048]{4,3,5,0,2,1:T(8,128)(2,1)} fusion(f32[3,8,2048,96]{3,1,2,0:T(8,128)} %bitcast.49, f32[3,8,2048,96]{3,1,2,0:T(8,128)} %bitcast.48), kind=kLoop, calls=%fused_computation.3 | loop fusion | flops 9437184 | bytes 47185920 | tf_op jit(solution)/shard_map/reshape | solution.py:46
  501.4 15.5 %copy.60 = bf16[3,1,1,8,96,2048]{5,4,3,2,1,0:T(8,128)(2,1)} copy(bf16[3,1,1,8,96,2048]{4,3,5,0,2,1:T(8,128)(2,1)} %fusion) | data formatting | bytes 18874368
  (16 shorter events, 3.0 us)
Async XLA Ops:
  0.6 8.8 %copy-start = (bf16[4,512,768]{2,1,0:T(8,128)(2,1)S(1)}, bf16[4,512,768]{2,1,0:T(8,128)(2,1)}, u32[]{:S(2)}) copy-start(bf16[4,512,768]{2,1,0:T(8,128)(2,1)} %param.7) | copy-start | bytes 9437188
  24.5 11.9 %copy-start.1 = (s32[128]{0:T(128)S(1)}, s32[128]{0:T(128)}, u32[]{:S(2)}) copy-start(s32[128]{0:T(128)} %param.8) | copy-start | bytes 1540
  24.5 11.9 %copy-start.2 = (s32[128]{0:T(128)S(1)}, s32[128]{0:T(128)}, u32[]{:S(2)}) copy-start(s32[128]{0:T(128)} %param.9) | copy-start | bytes 1540
  24.5 133.4 %all-to-all-start = ((bf16[3,1,4,128,4,768]{5,4,2,0,1,3:T(4,128)(2,1)}), bf16[3,1,4,128,4,768]{5,4,2,0,1,3:T(4,128)(2,1)}, u32[]{:S(2)}, u32[]{:S(2)}) async-start(bf16[3,1,4,128,4,768]{5,4,2,0,1,3:T(4,128)(2,1)} %copy.49), calls=%async_computation | async-start | bytes 18874368 | tf_op jit(solution)/shard_map/all_to_all | solution.py:28
where the time goes:
time: 523 us; the launch traced here: 517 us
  local copies, waits for them, and re-layouts  155 us (30%)
  blocking collectives  149 us (28%)
  waiting for transfers between devices  121 us (23%)
  other arithmetic  78.9 us (15%)
  starting transfers between devices  11.9 us (2%)
    all_to_all x1, blocking collectives, per_device(): lax.all_to_all(outgoing, ('grp', 'sub'), split_axis=1, concat_axis=3, til...  149 us
    all_to_all x1, waiting for transfers between devices, per_device(): lax.all_to_all(pieces, ('grp', 'sub'), split_axis=3, concat_axis=1, tiled...  121 us
    unnamed x11, local copies, waits for them, and re-layouts  33.9 us
    gather x2, local copies, waits for them, and re-layouts, per_device(): ordered = jnp.take(received, picked, axis=1)  32.7 us
    convert_element_type x1, local copies, waits for them, and re-layouts, per_device(): placed.astype(jnp.float32)  22.3 us
    reshape x1, other arithmetic, per_device(): quantized = quantized.reshape(matrices, 1, 1, per_group, columns, full_rows)  21.2 us
    reduce_max x2, other arithmetic, per_device(): block_scale = jnp.max(jnp.abs(blocks), axis=3) + EPS  16 us
    all_to_all x1, local copies, waits for them, and re-layouts, per_device(): lax.all_to_all(outgoing, ('grp', 'sub'), split_axis=1, concat_axis=3, til...  15.7 us
  transfers between devices with their start and end apart: 1, of which 1 were waited for; matrix products, arithmetic and copies ran while one was open for 0% of the time, Pallas kernels for 0%

commit v1 on v0

v1 whole, which is shorter than its diff:
```python
import functools

import jax
import jax.numpy as jnp
from jax import lax
from jax.experimental import pallas as pl
from jax.experimental.pallas import tpu as pltpu
from jax.sharding import PartitionSpec as P

BLOCK = 128
EPS = 1e-06
MESH = pl.DeviceIdType.MESH
MATS = 3
HOPS = (1, 3, 2)


def move_kernel(index_ref, gate, up, down, out, *scratch):
    first = scratch[0:3]
    second = scratch[3:6]
    own = scratch[6]
    turned = scratch[7:10]
    middle = scratch[10:13]
    sorted_ = scratch[13:16]
    relay = scratch[16:19]
    own_sem, first_send, first_recv, second_send, second_recv = scratch[19:24]
    y_send, y_recv, third_send, third_recv, last_send, last_recv, keep_sem = scratch[24:31]
    weights = (gate, up, down)

    g = lax.axis_index("grp")
    q = lax.axis_index("sub")
    x, z, yl = g // 8, (g // 2) % 4, g % 2
    core = q % 2
    s8 = yl * 4 + q

    def device(xx, zz, ss):
        return ((xx * 4 + zz) * 2 + ss // 4, ss % 4)

    def pick(a, b):
        return jnp.where(core == 0, a, b)

    def flip(a, b):
        low = (a + b) % 2
        high = (a // 2 + b // 2) % 2
        return high * 2 + low

    x_to = [(x + d) % 4 for d in range(4)]
    z_to = [(z + d) % 4 for d in range(4)]
    x_from = [(x + 4 - d) % 4 for d in range(4)]
    z_from = [(z + 4 - d) % 4 for d in range(4)]
    dev1 = [device(pick(x, x_to[d]), pick(z_to[d], z), s8) for d in range(4)]
    dev2 = [device(pick(x_to[d], x), pick(z, z_to[d]), s8) for d in range(4)]
    s8_to = [(flip((s8 // 4) * 2 + (s8 // 2) % 2, r // 2)) * 2 + (s8 + r) % 2 for r in range(8)]
    dev_y = [device(x, z, s8_to[r]) for r in range(8)]

    barrier = pltpu.get_barrier_semaphore()
    partners = dev1[1:] + dev2[1:] + dev_y[1:]
    for partner in partners:
        pl.semaphore_signal(barrier, inc=1, device_id=partner, device_id_type=MESH)
    pl.semaphore_wait(barrier, len(partners))

    tile2 = [pick(flip(q, x_to[d]), z_to[d]) for d in range(4)]

    def source(m, d1, t):
        slot = pick(t, flip(q, x_to[d1]))
        block = pick(z_to[d1], t)
        return weights[m].at[slot, pl.ds(pl.multiple_of(block * BLOCK, BLOCK), BLOCK), :]

    def first_copy(m, d1, d2):
        t = tile2[d2]
        return pltpu.make_async_remote_copy(
            src_ref=source(m, d1, t),
            dst_ref=first[m].at[d1 - 1, t],
            send_sem=first_send.at[m],
            recv_sem=first_recv.at[m, d1 - 1, t],
            device_id=dev1[d1],
            device_id_type=MESH,
        )

    def second_copy(m, d1, d2):
        t = tile2[d2]
        return pltpu.make_async_remote_copy(
            src_ref=source(m, 0, t) if d1 == 0 else first[m].at[d1 - 1, t],
            dst_ref=second[m].at[d2 - 1, d1],
            send_sem=second_send.at[m],
            recv_sem=second_recv.at[m, d2 - 1, d1],
            device_id=dev2[d2],
            device_id_type=MESH,
        )

    def own_copy(m):
        return pltpu.make_async_copy(source(m, 0, tile2[0]), own.at[m], own_sem.at[m])

    def start_first(m):
        for d2 in (1, 3, 2, 0):
            for d1 in HOPS:
                first_copy(m, d1, d2).start()
        for d2 in HOPS:
            second_copy(m, 0, d2).start()
        own_copy(m).start()

    def forward(m):
        for d2 in (1, 3, 2, 0):
            for d1 in HOPS:
                first_copy(m, d1, d2).wait_recv()
                if d2:
                    second_copy(m, d1, d2).start()

    units, columns = turned[0].shape[1], turned[0].shape[2]

    def y_copy(m, r):
        return pltpu.make_async_remote_copy(
            src_ref=turned[m].at[:, s8_to[r]],
            dst_ref=middle[m].at[pl.ds(s8 * 16, 16)],
            send_sem=y_send.at[m],
            recv_sem=y_recv.at[m, r - 1],
            device_id=dev_y[r],
            device_id_type=MESH,
        )

    def place_of(d1, d2):
        return pick(x_from[d2] * 4 + z_from[d1], x_from[d1] * 4 + z_from[d2])

    def turn_and_cross(m):
        own_copy(m).wait()

        def turn(tile, place):
            turned[m][place] = tile.T.reshape(units, columns, BLOCK)

        turn(own[m], place_of(0, 0))
        for d1 in HOPS:
            turn(first[m][d1 - 1, tile2[0]], place_of(d1, 0))
        for d1 in (0,) + HOPS:
            for d2 in HOPS:
                second_copy(m, d1, d2).wait_recv()
                turn(second[m][d2 - 1, d1], place_of(d1, d2))
        for r in range(1, 8):
            y_copy(m, r).start()
        middle[m][pl.ds(s8 * 16, 16)] = turned[m][:, s8]

    def third_copy(m, d1, t):
        return pltpu.make_async_remote_copy(
            src_ref=sorted_[m].at[pick(t, x_to[d1]), pick(z_to[d1], t)],
            dst_ref=relay[m].at[d1 - 1, t],
            send_sem=third_send.at[m],
            recv_sem=third_recv.at[m, d1 - 1, t],
            device_id=dev1[d1],
            device_id_type=MESH,
        )

    def last_source(m, d1, d2):
        t = pick(x_to[d2], z_to[d2])
        if d1 == 0:
            return sorted_[m].at[pick(t, x), pick(z, t)]
        return relay[m].at[d1 - 1, t]

    def last_place(m, d1):
        return out.at[m, pick(x * 4 + z_from[d1], x_from[d1] * 4 + z)]

    def last_copy(m, d1, d2):
        return pltpu.make_async_remote_copy(
            src_ref=last_source(m, d1, d2),
            dst_ref=last_place(m, d1),
            send_sem=last_send.at[m],
            recv_sem=last_recv.at[m],
            device_id=dev2[d2],
            device_id_type=MESH,
        )

    def keep_copy(m, d1):
        return pltpu.make_async_copy(last_source(m, d1, 0), last_place(m, d1), keep_sem.at[m, d1])

    def third_tile(d2):
        return pick(x_to[d2], z_to[d2])

    def permute(m):
        for r in range(1, 8):
            y_copy(m, r).wait_recv()

        def step(t, carry):
            for k in range(8):
                sorted_[m][t // 4, t % 4, k] = middle[m][index_ref[t * 8 + k]]
            return carry

        lax.fori_loop(0, 16, step, 0)
        for d2 in (1, 3, 2, 0):
            for d1 in HOPS:
                third_copy(m, d1, third_tile(d2)).start()
        for d2 in HOPS:
            last_copy(m, 0, d2).start()
        keep_copy(m, 0).start()

    def finish(m):
        for d2 in (1, 3, 2, 0):
            for d1 in HOPS:
                third_copy(m, d1, third_tile(d2)).wait_recv()
                if d2:
                    last_copy(m, d1, d2).start()
                else:
                    keep_copy(m, d1).start()

    start_first(0)
    start_first(1)
    start_first(2)
    forward(0)
    forward(1)
    turn_and_cross(0)
    forward(2)
    turn_and_cross(1)
    permute(0)
    turn_and_cross(2)
    finish(0)
    permute(1)
    finish(1)
    permute(2)
    finish(2)

    def drain(ref, sem):
        pltpu.make_async_copy(ref, ref, sem).wait()

    for m in range(MATS):
        drain(first[m], first_send.at[m])
        drain(second[m], second_send.at[m])
        drain(middle[m].at[pl.ds(0, 112)], y_send.at[m])
        drain(relay[m], third_send.at[m])
        drain(relay[m], last_send.at[m])
        drain(relay[m], last_recv.at[m])
        for d1 in range(4):
            keep_copy(m, d1).wait()


def scale_kernel(low_ref, moved, packed, scales):
    blocks = moved.shape[1]
    columns = moved.shape[3]
    k = pl.program_id(1)
    low = low_ref[k]
    found = []
    for b in range(blocks):
        place = ((b // 4) ^ low) * 4 + b % 4
        values = moved[0, place, 0].astype(jnp.float32)
        scale = jnp.max(jnp.abs(values), axis=1, keepdims=True) + EPS
        packed[0, 0, 0, 0, :, b * BLOCK : (b + 1) * BLOCK] = (values * (1.0 / scale)).astype(jnp.bfloat16)
        found.append(scale)
    scales[0, 0] = jnp.concatenate(found, axis=1).T


def per_device(gate, up, down, source_order, target_order):
    slots, rows, hidden = gate.shape
    columns = hidden // 8
    experts = source_order.shape[0]
    matches = (source_order[None, :] == target_order[:, None]).astype(jnp.int32)
    picked = jnp.sum(matches * jnp.arange(experts, dtype=jnp.int32)[None, :], axis=1)
    g = lax.axis_index("grp")
    x = g // 8
    col, yl, low = picked // 8, (picked // 4) % 2, picked % 4
    index = (yl * 4 + (low ^ x)) * 16 + col

    tile = (BLOCK, hidden)
    brick = (columns, BLOCK)
    bf16 = jnp.bfloat16
    dma = pltpu.SemaphoreType.DMA
    any_space = pl.BlockSpec(memory_space=pl.ANY)
    scratch = (
        [pltpu.VMEM((3, 4) + tile, bf16)] * 3
        + [pltpu.VMEM((3, 4) + tile, bf16)] * 3
        + [pltpu.VMEM((3,) + tile, bf16)]
        + [pltpu.VMEM((16, 8) + brick, bf16)] * 3
        + [pltpu.VMEM((128,) + brick, bf16)] * 3
        + [pltpu.VMEM((4, 4, 8) + brick, bf16)] * 3
        + [pltpu.VMEM((3, 4, 8) + brick, bf16)] * 3
        + [dma((3,)), dma((3,)), dma((3, 3, 4)), dma((3,)), dma((3, 3, 4))]
        + [dma((3,)), dma((3, 7)), dma((3,)), dma((3, 3, 4)), dma((3,)), dma((3,)), dma((3, 4))]
    )
    moved = pl.pallas_call(
        move_kernel,
        out_shape=jax.ShapeDtypeStruct((3, 16, 8) + brick, bf16),
        in_specs=[pl.BlockSpec(memory_space=pltpu.SMEM), any_space, any_space, any_space],
        out_specs=any_space,
        scratch_shapes=scratch,
        compiler_params=pltpu.CompilerParams(
            collective_id=0, has_side_effects=True, vmem_limit_bytes=60 * 2**20
        ),
        name="move",
    )(index, gate, up, down)

    mine = lax.dynamic_slice(low, ((g // 2) * 8,), (8,))
    packed, found = pl.pallas_call(
        scale_kernel,
        grid_spec=pltpu.PrefetchScalarGridSpec(
            num_scalar_prefetch=1,
            grid=(3, 8),
            in_specs=[pl.BlockSpec((1, 16, 1) + brick, lambda m, k, low: (m, 0, k, 0, 0))],
            out_specs=[
                pl.BlockSpec((1, 1, 1, 1, columns, 16 * BLOCK), lambda m, k, low: (m, 0, 0, k, 0, 0)),
                pl.BlockSpec((1, 1, 16, columns), lambda m, k, low: (m, k, 0, 0)),
            ],
        ),
        out_shape=[
            jax.ShapeDtypeStruct((3, 1, 1, 8, columns, 16 * BLOCK), bf16),
            jax.ShapeDtypeStruct((3, 8, 16, columns), jnp.float32),
        ],
        name="scale",
    )(mine, moved)
    scales = found.transpose(0, 2, 1, 3).reshape(3, 1, 1, 16, hidden)
    return packed, scales


def solution(mesh):
    placed = (P("grp", "sub", None), P("grp", "sub", None), P("grp", "sub", None), P(), P())
    return jax.shard_map(
        per_device,
        mesh=mesh,
        in_specs=placed,
        out_specs=(P(None, "grp", "sub", None, None, None), P(None, "grp", "sub", None, None)),
        check_vma=False,
    )
```

time: 523 us -> 250 us (0.48); the launches traced: 517 us -> 250 us
  Pallas kernels: 0 us -> 245 us
  local copies, waits for them, and re-layouts: 155 us -> 2.41 us
  blocking collectives: 149 us -> 0 us
  waiting for transfers between devices: 121 us -> 0 us
  other arithmetic: 78.9 us -> 1.38 us
  starting transfers between devices: 11.9 us -> 0 us
    pallas_call x0 -> x2, Pallas kernels: none -> 245 us  [the longest x1 226 us: per_device(): pl.pallas_call(move_kernel, out_shape=jax.ShapeDtypeStruct((3, 16, 8) + b...]
    all_to_all x1 -> x0, blocking collectives: 149 us -> none  [per_device(): lax.all_to_all(outgoing, ('grp', 'sub'), split_axis=1, concat_axis=3, til...]
    all_to_all x1 -> x0, waiting for transfers between devices: 121 us -> none  [per_device(): lax.all_to_all(pieces, ('grp', 'sub'), split_axis=3, concat_axis=1, tiled...]
    unnamed x11 -> x0, local copies, waits for them, and re-layouts: 33.9 us -> none
    gather x2 -> x0, local copies, waits for them, and re-layouts: 32.7 us -> none  [per_device(): ordered = jnp.take(received, picked, axis=1)]
    convert_element_type x1 -> x0, local copies, waits for them, and re-layouts: 22.3 us -> none  [per_device(): placed.astype(jnp.float32)]
    reshape x1 -> x0, other arithmetic: 21.2 us -> none  [per_device(): quantized = quantized.reshape(matrices, 1, 1, per_group, columns, full_rows)]
    reshape x3 -> x1, local copies, waits for them, and re-layouts: 18.1 us -> 0.77 us  [per_device(): scales = found.transpose(0, 2, 1, 3).reshape(3, 1, 1, 16, hidden)]
  transfers between devices with their start and end apart: 1 -> 0, of which waited for: 1 -> 0; matrix products, arithmetic and copies ran while one was open for 0% -> 0% of each run, Pallas kernels for 0% -> 0%
where the time goes in v1:
time: 250 us
  Pallas kernels  245 us (98%)
    pallas_call x1, Pallas kernels, per_device(): pl.pallas_call(move_kernel, out_shape=jax.ShapeDtypeStruct((3, 16, 8) + b...  226 us
    pallas_call x1, Pallas kernels, per_device(): pl.pallas_call(scale_kernel, grid_spec=pltpu.PrefetchScalarGridSpec(num_s...  19.6 us

profile of v1, /device:TPU:1, one launch (start us, length us, event | category | flops | bytes accessed | tf_op | source)
XLA Modules:
  0.0 249.9 jit_solution(2221456490599317928)
XLA Ops:
  0.7 0.8 select_reduce_fusion
  1.5 0.5 multiply_add_fusion
  2.0 0.6 dynamic_slice.3.low_ref
  2.7 225.8 %move.1.moved = bf16[3,16,8,96,128]{4,3,2,1,0:T(8,128)(2,1)} custom-call(s32[128]{0:T(128)} %get-tuple-element.10.index_ref, bf16[4,512,768]{2,1,0:T(8,128)(2,1)} %gate.1, bf16[4,512,768]{2,1,0:T(8,128)(2,1)} %up.1, bf16[4,512,768]{2,1,0:T(8,128)(2,1)} %down.1), custom_call_target="tpu_custom_call" | custom-call | tf_op jit(solution)/shard_map/move/pallas_call | solution.py:273
  228.5 19.6 %scale.1 = (bf16[3,1,1,8,96,2048]{5,4,3,2,1,0:T(8,128)(2,1)}, f32[3,8,16,96]{3,2,1,0:T(8,128)}) custom-call(s32[8]{0:T(128)} %dynamic_slice.3.low_ref, bf16[3,16,8,96,128]{4,3,2,1,0:T(8,128)(2,1)} %move.1.moved), custom_call_target="tpu_custom_call" | custom-call | tf_op jit(solution)/shard_map/scale/pallas_call | solution.py:286
  248.1 1.0 copy.9
  249.1 0.8 reshape.9

commit v2 on v1

--- a/solution.py
+++ b/solution.py
@@ -228,19 +228,34 @@
             keep_copy(m, d1).wait()
 
 
-def scale_kernel(low_ref, moved, packed, scales):
-    blocks = moved.shape[1]
+def scale_kernel(low_ref, moved, packed, scales, ready, found, sem):
     columns = moved.shape[3]
-    k = pl.program_id(1)
-    low = low_ref[k]
-    found = []
-    for b in range(blocks):
-        place = ((b // 4) ^ low) * 4 + b % 4
-        values = moved[0, place, 0].astype(jnp.float32)
-        scale = jnp.max(jnp.abs(values), axis=1, keepdims=True) + EPS
-        packed[0, 0, 0, 0, :, b * BLOCK : (b + 1) * BLOCK] = (values * (1.0 / scale)).astype(jnp.bfloat16)
-        found.append(scale)
-    scales[0, 0] = jnp.concatenate(found, axis=1).T
+    lane = lax.broadcasted_iota(jnp.int32, (columns, BLOCK), 1)
+
+    def out_copy(m, k):
+        return pltpu.make_async_copy(ready.at[m, k], packed.at[m, 0, 0, k], sem.at[m, k])
+
+    for m in range(MATS):
+
+        def step(k, carry):
+            low = low_ref[k]
+            seen = jnp.zeros((columns, BLOCK), jnp.float32)
+            for b in range(16):
+                place = ((b // 4) ^ low) * 4 + b % 4
+                values = moved[m, place, k].astype(jnp.float32)
+                scale = jnp.max(jnp.abs(values), axis=1, keepdims=True) + EPS
+                ready[m, k, :, b * BLOCK : (b + 1) * BLOCK] = (values * (1.0 / scale)).astype(jnp.bfloat16)
+                seen = jnp.where(lane == b, scale, seen)
+            found[k] = seen.T[:16]
+            out_copy(m, k).start()
+            return carry
+
+        lax.fori_loop(0, 8, step, 0)
+        scales[m, 0, 0] = jnp.concatenate([found[k] for k in range(8)], axis=1)
+
+    for m in range(MATS):
+        for k in range(8):
+            out_copy(m, k).wait()
 
 
 def per_device(gate, up, down, source_order, target_order):
@@ -272,36 +287,29 @@
     )
     moved = pl.pallas_call(
         move_kernel,
-        out_shape=jax.ShapeDtypeStruct((3, 16, 8) + brick, bf16),
+        out_shape=pltpu.VMEM((3, 16, 8) + brick, bf16),
         in_specs=[pl.BlockSpec(memory_space=pltpu.SMEM), any_space, any_space, any_space],
-        out_specs=any_space,
+        out_specs=pl.BlockSpec(memory_space=pltpu.VMEM),
         scratch_shapes=scratch,
         compiler_params=pltpu.CompilerParams(
-            collective_id=0, has_side_effects=True, vmem_limit_bytes=60 * 2**20
+            collective_id=0, has_side_effects=True, vmem_limit_bytes=51 * 2**20
         ),
         name="move",
     )(index, gate, up, down)
 
     mine = lax.dynamic_slice(low, ((g // 2) * 8,), (8,))
-    packed, found = pl.pallas_call(
+    return pl.pallas_call(
         scale_kernel,
-        grid_spec=pltpu.PrefetchScalarGridSpec(
-            num_scalar_prefetch=1,
-            grid=(3, 8),
-            in_specs=[pl.BlockSpec((1, 16, 1) + brick, lambda m, k, low: (m, 0, k, 0, 0))],
-            out_specs=[
-                pl.BlockSpec((1, 1, 1, 1, columns, 16 * BLOCK), lambda m, k, low: (m, 0, 0, k, 0, 0)),
-                pl.BlockSpec((1, 1, 16, columns), lambda m, k, low: (m, k, 0, 0)),
-            ],
-        ),
+        in_specs=[pl.BlockSpec(memory_space=pltpu.SMEM), pl.BlockSpec(memory_space=pltpu.VMEM)],
+        out_specs=[any_space, pl.BlockSpec(memory_space=pltpu.VMEM)],
         out_shape=[
             jax.ShapeDtypeStruct((3, 1, 1, 8, columns, 16 * BLOCK), bf16),
-            jax.ShapeDtypeStruct((3, 8, 16, columns), jnp.float32),
+            jax.ShapeDtypeStruct((3, 1, 1, 16, hidden), jnp.float32),
         ],
+        scratch_shapes=[pltpu.VMEM((3, 8, columns, 16 * BLOCK), bf16), pltpu.VMEM((8, 16, columns), jnp.float32), dma((3, 8))],
+        compiler_params=pltpu.CompilerParams(vmem_limit_bytes=20 * 2**20),
         name="scale",
     )(mine, moved)
-    scales = found.transpose(0, 2, 1, 3).reshape(3, 1, 1, 16, hidden)
-    return packed, scales
 
 
 def solution(mesh):

time: 250 us -> 238 us (0.952)
  Pallas kernels: 245 us -> 236 us
    pallas_call x2, Pallas kernels: 245 us -> 236 us  [the longest x1 225 us: per_device(): pl.pallas_call(move_kernel, out_shape=pltpu.VMEM((3, 16, 8) + brick, bf16...]
where the time goes in v2:
time: 238 us
  Pallas kernels  236 us (99%)
    pallas_call x1, Pallas kernels, per_device(): pl.pallas_call(move_kernel, out_shape=pltpu.VMEM((3, 16, 8) + brick, bf16...  225 us
    pallas_call x1, Pallas kernels, per_device(): pl.pallas_call(scale_kernel, in_specs=[pl.BlockSpec(memory_space=pltpu.SM...  10.2 us

profile of v2, /device:TPU:1, one launch (start us, length us, event | category | flops | bytes accessed | tf_op | source)
XLA Modules:
  0.0 237.9 jit_solution(11335186652717844623)
XLA Ops:
  0.7 0.8 select_reduce_fusion
  1.5 0.5 multiply_add_fusion
  2.0 0.1 dynamic_slice.3.low_ref
  2.1 225.5 %move.1.moved = bf16[3,16,8,96,128]{4,3,2,1,0:T(8,128)(2,1)S(1)} custom-call(s32[128]{0:T(128)} %get-tuple-element.2.index_ref, bf16[4,512,768]{2,1,0:T(8,128)(2,1)} %gate.1, bf16[4,512,768]{2,1,0:T(8,128)(2,1)} %up.1, bf16[4,512,768]{2,1,0:T(8,128)(2,1)} %down.1), custom_call_target="tpu_custom_call" | custom-call | tf_op jit(solution)/shard_map/move/pallas_call | solution.py:288
  227.6 10.2 %scale.1 = (bf16[3,1,1,8,96,2048]{5,4,3,2,1,0:T(8,128)(2,1)}, f32[3,1,1,16,768]{4,3,2,1,0:T(8,128)}) custom-call(s32[8]{0:T(128)S(1)} %dynamic_slice.3.low_ref, bf16[3,16,8,96,128]{4,3,2,1,0:T(8,128)(2,1)S(1)} %move.1.moved), custom_call_target="tpu_custom_call" | custom-call | tf_op jit(solution)/shard_map/scale/pallas_call | solution.py:301

commit v3 on v2

--- a/solution.py
+++ b/solution.py
@@ -12,6 +12,343 @@
 MESH = pl.DeviceIdType.MESH
 MATS = 3
 HOPS = (1, 3, 2)
+ROOMS = ((12, 11), (13, 12), (14, 14))
+
+
+def device(x, z, s8):
+    return ((x * 4 + z) * 2 + s8 // 4, s8 % 4)
+
+
+def flip(a, b):
+    low = (a + b) % 2
+    high = (a // 2 + b // 2) % 2
+    return high * 2 + low
+
+
+def place():
+    g = lax.axis_index("grp")
+    q = lax.axis_index("sub")
+    return g // 8, (g // 2) % 4, g % 2, q
+
+
+def greet(partners):
+    barrier = pltpu.get_barrier_semaphore()
+    for partner in partners:
+        pl.semaphore_signal(barrier, inc=1, device_id=partner, device_id_type=MESH)
+    pl.semaphore_wait(barrier, len(partners))
+
+
+def drain(ref, sem):
+    pltpu.make_async_copy(ref, ref, sem).wait()
+
+
+def crossings(s8):
+    return [flip((s8 // 4) * 2 + (s8 // 2) % 2, r // 2) * 2 + (s8 + r) % 2 for r in range(8)]
+
+
+def plan_kernel(source_ref, target_ref, table_ref, level_ref):
+    x, z, _, _ = place()
+    f32, i32 = jnp.float32, jnp.int32
+    shape = (128, 128)
+    row = lax.broadcasted_iota(i32, shape, 0)
+    lane = lax.broadcasted_iota(i32, shape, 1)
+    source = jnp.broadcast_to(source_ref[...].astype(f32), shape).T
+    target = jnp.broadcast_to(target_ref[...].astype(f32), shape)
+    found = jnp.where(source == target, lane.astype(f32), 0.0)
+    to = jnp.broadcast_to(jnp.sum(found, axis=1, keepdims=True), shape).astype(i32)
+    x_to, z_to = to // 32, (to // 8) % 4
+    x_at, z_at = row // 32, (row // 8) % 4
+    inner = ((row // 4) % 2) * 32 + row % 4
+
+    def down(values):
+        return jnp.sum(values.astype(f32), axis=0, keepdims=True).astype(i32)
+
+    worst = [jnp.zeros(shape, f32)] * 2
+    for kind in range(2):
+        at, end, mine = (x_at, x_to, x) if kind == 0 else (z_at, z_to, z)
+        key = (at * 4 + end).astype(f32)
+        same = jnp.where((key == key.T) & (lane < row), 1.0, 0.0)
+        rank = jnp.broadcast_to(jnp.sum(same, axis=1, keepdims=True), shape).astype(i32)
+        away = (end - at + 4) % 4
+        index = kind * 64 + inner + (z_at if kind == 0 else x_at) * 4
+        sent = (at == mine) & (away == lane // 32 + 1) & (rank == lane % 32)
+        step = lane // 8
+        if kind == 0:
+            slot = (x * 4 + (z + step) % 4) * 8 + lane % 8
+        else:
+            slot = (((x + step) % 4) * 4 + z) * 8 + lane % 8
+        got = (to == slot) & (lane < 32)
+        base = kind * 5
+        table_ref[base : base + 1, :] = down(jnp.where(sent, index, 0))
+        table_ref[base + 1 : base + 2, :] = down(jnp.where(got & (away == 0), index, 0))
+        table_ref[base + 2 : base + 3, :] = down(jnp.where(got & (away > 0), away - 1, 0))
+        table_ref[base + 3 : base + 4, :] = down(jnp.where(got & (away > 0), rank, 0))
+        table_ref[base + 4 : base + 5, :] = down(jnp.where(got & (away == 0), 1, 0))
+        needed = (rank + 1).astype(f32)
+        worst[0] = jnp.maximum(worst[0], jnp.where(away % 2 == 1, needed, 0.0))
+        worst[1] = jnp.maximum(worst[1], jnp.where(away == 2, needed, 0.0))
+    table_ref[10:16, :] = jnp.zeros((6, 128), i32)
+    side, across = (jnp.max(values) for values in worst)
+    level = jnp.int32(0)
+    for near, far in ROOMS:
+        level += ((side > near) | (across > far)).astype(i32)
+    level_ref[0] = level
+
+
+def quantize(load, store, columns):
+    lane = lax.broadcasted_iota(jnp.int32, (columns, BLOCK), 1)
+    seen = jnp.zeros((columns, BLOCK), jnp.float32)
+    for b in range(16):
+        values = load(b).astype(jnp.float32)
+        scale = jnp.max(jnp.abs(values), axis=1, keepdims=True) + EPS
+        store(b, (values * (1.0 / scale)).astype(jnp.bfloat16))
+        seen = jnp.where(lane == b, scale, seen)
+    return seen.T[:16]
+
+
+def direct_kernel(room, table, gate, up, down, out, scales, *scratch):
+    first = scratch[0:3]
+    own = scratch[3]
+    turned = scratch[4:7]
+    middle = scratch[7:10]
+    packs = scratch[10:12]
+    landed = scratch[12:15]
+    found = scratch[15]
+    own_sem, first_send, first_recv, y_send, y_recv = scratch[16:21]
+    direct_send, direct_recv, last_send, last_recv = scratch[21:25]
+    weights = (gate, up, down)
+    slots = (0, room[0], room[1], room[0])
+
+    def drain_direct(m):
+        for kind in range(2):
+            for d in HOPS:
+                drain(packs[0].at[kind, d - 1, pl.ds(0, slots[d])], direct_send.at[m, kind, d - 1])
+
+    x, z, yl, q = place()
+    core = q % 2
+    s8 = yl * 4 + q
+    units, columns = turned[0].shape[1], turned[0].shape[2]
+
+    def pick(a, b):
+        return jnp.where(core == 0, a, b)
+
+    x_to = [device((x + d) % 4, z, s8) for d in range(4)]
+    z_to = [device(x, (z + d) % 4, s8) for d in range(4)]
+    s8_to = crossings(s8)
+    y_to = [device(x, z, s) for s in s8_to]
+    greet(x_to[1:] + z_to[1:] + y_to[1:])
+
+    spot = pick(z, x)
+
+    def rows(m, d):
+        block = (spot + d) % 4
+        return weights[m].at[:, pl.ds(pl.multiple_of(block * BLOCK, BLOCK), BLOCK), :]
+
+    def first_copy(m, d):
+        return pltpu.make_async_remote_copy(
+            src_ref=rows(m, d),
+            dst_ref=first[m].at[d - 1],
+            send_sem=first_send.at[m],
+            recv_sem=first_recv.at[m, d - 1],
+            device_id=tuple(pick(a, b) for a, b in zip(z_to[d], x_to[d])),
+            device_id_type=MESH,
+        )
+
+    def own_copy(m):
+        return pltpu.make_async_copy(rows(m, 0), own.at[m], own_sem.at[m])
+
+    slot = (core * 4 + yl * 2 + q // 2) * 16
+
+    def origin(d):
+        return ((spot + 4 - d) % 4) * 4
+
+    def y_copy(m, d, r):
+        return pltpu.make_async_remote_copy(
+            src_ref=turned[m].at[pl.ds(origin(d), 4), s8_to[r]],
+            dst_ref=middle[m].at[pl.ds(slot + origin(d), 4)],
+            send_sem=y_send.at[m],
+            recv_sem=y_recv.at[m, r - 1],
+            device_id=y_to[r],
+            device_id_type=MESH,
+        )
+
+    def direct_copy(m, kind, d):
+        return pltpu.make_async_remote_copy(
+            src_ref=packs[m % 2].at[kind, d - 1, pl.ds(0, slots[d])],
+            dst_ref=landed[m].at[kind, d - 1, pl.ds(0, slots[d])],
+            send_sem=direct_send.at[m, kind, d - 1],
+            recv_sem=direct_recv.at[m, kind, d - 1],
+            device_id=(x_to, z_to)[kind][d],
+            device_id_type=MESH,
+        )
+
+    def last_copy(m, kind, d):
+        return pltpu.make_async_remote_copy(
+            src_ref=turned[m].at[pl.ds((kind * 3 + d - 1) * 2, 2)],
+            dst_ref=out.at[m, kind, (z, x)[kind]],
+            send_sem=last_send.at[m],
+            recv_sem=last_recv.at[m, kind, d - 1],
+            device_id=(z_to, x_to)[kind][d],
+            device_id_type=MESH,
+        )
+
+    def start(m):
+        for d in HOPS:
+            first_copy(m, d).start()
+        own_copy(m).start()
+
+    def turn(m, d):
+        if d:
+            first_copy(m, d).wait_recv()
+            tiles = first[m].at[d - 1]
+        else:
+            own_copy(m).wait()
+            tiles = own.at[m]
+
+        def one(i, carry):
+            turned[m][origin(d) + i] = tiles[i].T.reshape(units, columns, BLOCK)
+            return carry
+
+        lax.fori_loop(0, 4, one, 0)
+        for r in (2, 4, 6, 3, 5, 7, 1):
+            y_copy(m, d, r).start()
+        middle[m][pl.ds(slot + origin(d), 4)] = turned[m][pl.ds(origin(d), 4), s8]
+
+    def gather(m):
+        for r in range(1, 8):
+            drain(middle[m].at[pl.ds(0, 16)], y_recv.at[m, r - 1])
+        if m == 2:
+            drain_direct(0)
+        for d in HOPS:
+            for kind in range(2):
+
+                def one(r, carry):
+                    index = table[kind * 5, (d - 1) * 32 + r]
+                    for half in range(2):
+                        packs[m % 2][kind, d - 1, r, half] = middle[m][index + 16 * half]
+                    return carry
+
+                lax.fori_loop(0, slots[d], one, 0)
+                direct_copy(m, kind, d).start()
+
+    def spread(m):
+        for kind in range(2):
+            for d in HOPS:
+                direct_copy(m, kind, d).wait_recv()
+        drain(turned[m].at[pl.ds(0, 14)], y_send.at[m])
+        for d in HOPS + (0,):
+            for kind in range(2):
+
+                def one(k, carry):
+                    spot_in = d * 8 + k
+                    near = table[kind * 5 + 1, spot_in]
+                    hop = table[kind * 5 + 2, spot_in]
+                    rank = table[kind * 5 + 3, spot_in]
+                    stay = table[kind * 5 + 4, spot_in] > 0
+                    for half in range(2):
+                        here = middle[m][near + 16 * half]
+                        there = landed[m][kind, hop, rank, half]
+                        brick = lax.select(jnp.broadcast_to(stay, here.shape), here, there)
+                        if d == 0:
+                            out[m, kind, (z, x)[kind], half, k] = brick
+                        else:
+                            turned[m][(kind * 3 + d - 1) * 2 + half, k] = brick
+                    return carry
+
+                lax.fori_loop(0, 8, one, 0)
+                if d:
+                    last_copy(m, kind, d).start()
+
+    def settle(m):
+        for kind in range(2):
+            for d in HOPS:
+                last_copy(m, kind, d).wait_recv()
+        if m == MATS - 1:
+            return
+
+        def one(k, carry):
+            def load(b):
+                return out[m, (b // 4) % 2, b % 4, b // 8, k]
+
+            def store(b, brick):
+                out[m, (b // 4) % 2, b % 4, b // 8, k] = brick
+
+            found[k] = quantize(load, store, columns)
+            return carry
+
+        lax.fori_loop(0, 8, one, 0)
+        scales[m] = jnp.concatenate([found[k] for k in range(8)], axis=1)
+
+    for m in range(MATS):
+        start(m)
+    turn(0, 0)
+    turn(1, 0)
+    for d in HOPS:
+        turn(0, d)
+    for d in HOPS:
+        turn(1, d)
+    turn(2, 0)
+    gather(0)
+    for d in HOPS:
+        turn(2, d)
+    gather(1)
+    spread(0)
+    gather(2)
+    spread(1)
+    settle(0)
+    spread(2)
+    settle(1)
+    settle(2)
+
+    for m in range(MATS):
+        drain(first[m], first_send.at[m])
+        if m:
+            drain_direct(m)
+        drain(turned[m].at[pl.ds(0, 12)], last_send.at[m])
+
+
+def write_kernel(moved, early, packed, scales, ready, found, early_sem, sem):
+    columns = moved.shape[-2]
+    last = MATS - 1
+
+    def early_copy(m, k, b):
+        return pltpu.make_async_copy(
+            moved.at[m, (b // 4) % 2, b % 4, b // 8, k],
+            packed.at[m, 0, 0, k, :, pl.ds(b * BLOCK, BLOCK)],
+            early_sem.at[m],
+        )
+
+    def late_copy(k):
+        return pltpu.make_async_copy(ready.at[k], packed.at[last, 0, 0, k], sem.at[k])
+
+    for m in range(last):
+
+        def issue(k, carry):
+            for b in range(16):
+                early_copy(m, k, b).start()
+            return carry
+
+        lax.fori_loop(0, 8, issue, 0)
+
+    def one(k, carry):
+        def load(b):
+            return moved[last, (b // 4) % 2, b % 4, b // 8, k]
+
+        def store(b, brick):
+            ready[k, :, b * BLOCK : (b + 1) * BLOCK] = brick
+
+        found[k] = quantize(load, store, columns)
+        late_copy(k).start()
+        return carry
+
+    lax.fori_loop(0, 8, one, 0)
+    for m in range(last):
+        scales[m, 0, 0] = early[m]
+    scales[last, 0, 0] = jnp.concatenate([found[k] for k in range(8)], axis=1)
+    for m in range(last):
+        drain(packed.at[m], early_sem.at[m])
+    for k in range(8):
+        late_copy(k).wait()
 
 
 def move_kernel(index_ref, gate, up, down, out, *scratch):
@@ -258,7 +595,7 @@
             out_copy(m, k).wait()
 
 
-def per_device(gate, up, down, source_order, target_order):
+def through(table, gate, up, down, source_order, target_order):
     slots, rows, hidden = gate.shape
     columns = hidden // 8
     experts = source_order.shape[0]
@@ -292,7 +629,7 @@
         out_specs=pl.BlockSpec(memory_space=pltpu.VMEM),
         scratch_shapes=scratch,
         compiler_params=pltpu.CompilerParams(
-            collective_id=0, has_side_effects=True, vmem_limit_bytes=51 * 2**20
+            collective_id=2, has_side_effects=True, vmem_limit_bytes=51 * 2**20
         ),
         name="move",
     )(index, gate, up, down)
@@ -312,6 +649,75 @@
     )(mine, moved)
 
 
+def per_device(gate, up, down, source_order, target_order):
+    slots, rows, hidden = gate.shape
+    columns = hidden // 8
+    tile = (BLOCK, hidden)
+    brick = (columns, BLOCK)
+    bf16, f32 = jnp.bfloat16, jnp.float32
+    dma = pltpu.SemaphoreType.DMA
+    any_space = pl.BlockSpec(memory_space=pl.ANY)
+    smem = pl.BlockSpec(memory_space=pltpu.SMEM)
+    vmem = pl.BlockSpec(memory_space=pltpu.VMEM)
+    results = [
+        jax.ShapeDtypeStruct((3, 1, 1, 8, columns, 16 * BLOCK), bf16),
+        jax.ShapeDtypeStruct((3, 1, 1, 16, hidden), f32),
+    ]
+
+    table, level = pl.pallas_call(
+        plan_kernel,
+        out_shape=[
+            jax.ShapeDtypeStruct((16, 128), jnp.int32),
+            jax.ShapeDtypeStruct((1,), jnp.int32),
+        ],
+        in_specs=[vmem, vmem],
+        out_specs=[vmem, smem],
+        name="plan",
+    )(source_order[None, :], target_order[None, :])
+
+    def direct(room, number, table, gate, up, down, source_order, target_order):
+        scratch = (
+            [pltpu.VMEM((3, 4) + tile, bf16)] * 3
+            + [pltpu.VMEM((3, 4) + tile, bf16)]
+            + [pltpu.VMEM((16, 8) + brick, bf16)] * 3
+            + [pltpu.VMEM((128,) + brick, bf16)] * 3
+            + [pltpu.VMEM((2, 3, max(room), 2) + brick, bf16)] * 2
+            + [pltpu.VMEM((2, 3, max(room), 2) + brick, bf16)] * 3
+            + [pltpu.VMEM((8, 16, columns), f32)]
+            + [dma((3,)), dma((3,)), dma((3, 3)), dma((3,)), dma((3, 7))]
+            + [dma((3, 2, 3)), dma((3, 2, 3)), dma((3,)), dma((3, 2, 3))]
+        )
+        moved, early = pl.pallas_call(
+            functools.partial(direct_kernel, room),
+            out_shape=[pltpu.VMEM((3, 2, 4, 2, 8) + brick, bf16), pltpu.VMEM((2, 16, hidden), f32)],
+            in_specs=[smem, any_space, any_space, any_space],
+            out_specs=[vmem, vmem],
+            scratch_shapes=scratch,
+            compiler_params=pltpu.CompilerParams(
+                collective_id=number, has_side_effects=True, vmem_limit_bytes=50 * 2**20
+            ),
+            name="direct",
+        )(table, gate, up, down)
+        return pl.pallas_call(
+            write_kernel,
+            in_specs=[vmem, vmem],
+            out_specs=[any_space, vmem],
+            out_shape=results,
+            scratch_shapes=[
+                pltpu.VMEM((8, columns, 16 * BLOCK), bf16),
+                pltpu.VMEM((8, 16, columns), f32),
+                dma((2,)),
+                dma((8,)),
+            ],
+            compiler_params=pltpu.CompilerParams(vmem_limit_bytes=12 * 2**20),
+            name="write",
+        )(moved, early)
+
+    operands = (table, gate, up, down, source_order, target_order)
+    ways = [functools.partial(direct, room, 3 + i) for i, room in enumerate(ROOMS)]
+    return tuple(lax.switch(level[0], ways + [through], *operands))
+
+
 def solution(mesh):
     placed = (P("grp", "sub", None), P("grp", "sub", None), P("grp", "sub", None), P(), P())
     return jax.shard_map(

time: 238 us -> 193 us (0.81)
  Pallas kernels: 236 us -> 191 us
    pallas_call x2 -> x3, Pallas kernels: 236 us -> 191 us  [the longest x1 185 us: direct(): pl.pallas_call(functools.partial(direct_kernel, room), out_shape=[pltpu.V...]
where the time goes in v3:
time: 193 us
  Pallas kernels  191 us (99%)
    pallas_call x1, Pallas kernels, direct(): pl.pallas_call(functools.partial(direct_kernel, room), out_shape=[pltpu.V...  185 us
    pallas_call x1, Pallas kernels, direct(): pl.pallas_call(write_kernel, in_specs=[vmem, vmem], out_specs=[any_space,...  4.71 us

profile of v3, /device:TPU:1, one launch (start us, length us, event | category | flops | bytes accessed | tf_op | source)
XLA Modules:
  0.0 192.9 jit_solution(3536230113306055702)
XLA Ops:
  0.6 1.8 plan.1
  3.1 189.6 %conditional.1 = ((bf16[3,1,1,8,96,2048]{5,4,3,2,1,0:T(8,128)(2,1)}, f32[3,1,1,16,768]{4,3,2,1,0:T(8,128)})) conditional(s32[]{:T(128)} %bitcast.2, (s32[16,128]{1,0:T(8,128)S(1)}, bf16[4,512,768]{2,1,0:T(8,128)(2,1)}, bf16[4,512,768]{2,1,0:T(8,128)(2,1)}, bf16[4,512,768]{2,1,0:T(8,128)(2,1)}) %tuple.19, ...), branch_computations={%region_0.0_spmd, %region_1.0_spmd, %region_2.0_spmd, %region_3.5_... | conditional | flops 54816 | bytes 3483 | solution.py:718
  3.1 184.6 %direct.3 = (bf16[3,2,4,2,8,96,128]{6,5,4,3,2,1,0:T(8,128)(2,1)S(1)}, f32[2,16,768]{2,1,0:T(8,128)S(1)}) custom-call(s32[16,128]{1,0:T(8,128)S(1)} %get-tuple-element.34.table, bf16[4,512,768]{2,1,0:T(8,128)(2,1)} %get-tuple-element.35.gate, bf16[4,512,768]{2,1,0:T(8,128)(2,1)} %get-tuple-element.36.up, bf16[4,512,768]{2,1,0:T(8,128)(2,1)} %get-tuple-element.37.down), custom_call_target="tpu_custom_call" | custom-call | tf_op jit(solution)/shard_map/cond/branch_0_fun/direct/pallas_call | solution.py:690
  187.7 4.7 %write.3 = (bf16[3,1,1,8,96,2048]{5,4,3,2,1,0:T(8,128)(2,1)}, f32[3,1,1,16,768]{4,3,2,1,0:T(8,128)}) custom-call(bf16[3,2,4,2,8,96,128]{6,5,4,3,2,1,0:T(8,128)(2,1)S(1)} %get-tuple-element.38.moved, f32[2,16,768]{2,1,0:T(8,128)S(1)} %get-tuple-element.39.early), custom_call_target="tpu_custom_call" | custom-call | tf_op jit(solution)/shard_map/cond/branch_0_fun/write/pallas_call | solution.py:701

commit v4 on v3

--- a/solution.py
+++ b/solution.py
@@ -12,7 +12,7 @@
 MESH = pl.DeviceIdType.MESH
 MATS = 3
 HOPS = (1, 3, 2)
-ROOMS = ((12, 11), (13, 12), (14, 14))
+ROOMS = ((14, 6), (15, 7), (16, 8))
 
 
 def device(x, z, s8):
@@ -44,6 +44,12 @@
 
 def crossings(s8):
     return [flip((s8 // 4) * 2 + (s8 // 2) % 2, r // 2) * 2 + (s8 + r) % 2 for r in range(8)]
+
+
+def window(ahead, across, behind, most, through_most):
+    low = jnp.maximum(jnp.maximum(across - through_most, across + behind - most), 0)
+    high = jnp.minimum(jnp.minimum(across, through_most), most - ahead)
+    return low, high
 
 
 def plan_kernel(source_ref, target_ref, table_ref, level_ref):
@@ -63,36 +69,63 @@
     def down(values):
         return jnp.sum(values.astype(f32), axis=0, keepdims=True).astype(i32)
 
-    worst = [jnp.zeros(shape, f32)] * 2
+    kinds = []
+    misfit = [jnp.zeros(shape, f32)] * len(ROOMS)
     for kind in range(2):
-        at, end, mine = (x_at, x_to, x) if kind == 0 else (z_at, z_to, z)
-        key = (at * 4 + end).astype(f32)
-        same = jnp.where((key == key.T) & (lane < row), 1.0, 0.0)
-        rank = jnp.broadcast_to(jnp.sum(same, axis=1, keepdims=True), shape).astype(i32)
+        at, end = (x_at, x_to) if kind == 0 else (z_at, z_to)
         away = (end - at + 4) % 4
+        at_lane, away_lane = at.astype(f32).T, away.astype(f32).T
+        near = at_lane == at.astype(f32)
+
+        def count(which):
+            return jnp.broadcast_to(
+                jnp.sum(jnp.where(which, 1.0, 0.0), axis=1, keepdims=True), shape
+            ).astype(i32)
+
+        rank = count(near & (away_lane == away.astype(f32)) & (lane < row))
+        ahead, across, behind = (count(near & (away_lane == float(d))) for d in (1, 2, 3))
+        kinds.append((at, away, rank, ahead, across, behind))
+        for i, (most, through_most) in enumerate(ROOMS):
+            low, high = window(ahead, across, behind, most, through_most)
+            misfit[i] = jnp.maximum(misfit[i], jnp.where(low > high, 1.0, 0.0))
+    level = jnp.int32(0)
+    for bad in misfit:
+        level += jnp.max(bad).astype(i32)
+    level_ref[0] = level
+    most, through_most = jnp.int32(ROOMS[-1][0]), jnp.int32(ROOMS[-1][1])
+    for i in reversed(range(len(ROOMS) - 1)):
+        most = jnp.where(level <= i, ROOMS[i][0], most)
+        through_most = jnp.where(level <= i, ROOMS[i][1], through_most)
+
+    table_ref[8:16, :] = jnp.zeros((8, 128), i32)
+    for kind in range(2):
+        at, away, rank, ahead, across, behind = kinds[kind]
+        low, high = window(ahead, across, behind, most, through_most)
+        right = jnp.minimum(jnp.maximum((across + behind - ahead + 64) // 2 - 32, low), high)
+        back = jnp.where((away == 1) | ((away == 2) & (rank < right)), 0, 1)
+        slot = jnp.where(
+            away == 1,
+            right + rank,
+            jnp.where(away == 3, across - right + rank, jnp.where(rank < right, rank, rank - right)),
+        )
         index = kind * 64 + inner + (z_at if kind == 0 else x_at) * 4
-        sent = (at == mine) & (away == lane // 32 + 1) & (rank == lane % 32)
+        mine = x if kind == 0 else z
+        sent = (at == mine) & (away > 0) & (back == lane // 32) & (slot == lane % 32)
         step = lane // 8
         if kind == 0:
-            slot = (x * 4 + (z + step) % 4) * 8 + lane % 8
+            place_here = (x * 4 + (z + step) % 4) * 8 + lane % 8
         else:
-            slot = (((x + step) % 4) * 4 + z) * 8 + lane % 8
-        got = (to == slot) & (lane < 32)
+            place_here = (((x + step) % 4) * 4 + z) * 8 + lane % 8
+        got = (to == place_here) & (lane < 32)
+        moved = got & (away > 0)
         base = kind * 5
         table_ref[base : base + 1, :] = down(jnp.where(sent, index, 0))
         table_ref[base + 1 : base + 2, :] = down(jnp.where(got & (away == 0), index, 0))
-        table_ref[base + 2 : base + 3, :] = down(jnp.where(got & (away > 0), away - 1, 0))
-        table_ref[base + 3 : base + 4, :] = down(jnp.where(got & (away > 0), rank, 0))
+        table_ref[base + 2 : base + 3, :] = down(jnp.where(moved, back, 0))
+        table_ref[base + 3 : base + 4, :] = down(
+            jnp.where(moved, slot + jnp.where(away == 2, 64, 0), 0)
+        )
         table_ref[base + 4 : base + 5, :] = down(jnp.where(got & (away == 0), 1, 0))
-        needed = (rank + 1).astype(f32)
-        worst[0] = jnp.maximum(worst[0], jnp.where(away % 2 == 1, needed, 0.0))
-        worst[1] = jnp.maximum(worst[1], jnp.where(away == 2, needed, 0.0))
-    table_ref[10:16, :] = jnp.zeros((6, 128), i32)
-    side, across = (jnp.max(values) for values in worst)
-    level = jnp.int32(0)
-    for near, far in ROOMS:
-        level += ((side > near) | (across > far)).astype(i32)
-    level_ref[0] = level
 
 
 def quantize(load, store, columns):
@@ -115,14 +148,10 @@
     landed = scratch[12:15]
     found = scratch[15]
     own_sem, first_send, first_recv, y_send, y_recv = scratch[16:21]
-    direct_send, direct_recv, last_send, last_recv = scratch[21:25]
+    direct_send, direct_recv, onward_send, onward_recv, last_send, last_recv = scratch[21:27]
     weights = (gate, up, down)
-    slots = (0, room[0], room[1], room[0])
-
-    def drain_direct(m):
-        for kind in range(2):
-            for d in HOPS:
-                drain(packs[0].at[kind, d - 1, pl.ds(0, slots[d])], direct_send.at[m, kind, d - 1])
+    most, through_most = room
+    parts = ((0, through_most), (through_most, most - through_most))
 
     x, z, yl, q = place()
     core = q % 2
@@ -172,15 +201,28 @@
             device_id_type=MESH,
         )
 
-    def direct_copy(m, kind, d):
-        return pltpu.make_async_remote_copy(
-            src_ref=packs[m % 2].at[kind, d - 1, pl.ds(0, slots[d])],
-            dst_ref=landed[m].at[kind, d - 1, pl.ds(0, slots[d])],
-            send_sem=direct_send.at[m, kind, d - 1],
-            recv_sem=direct_recv.at[m, kind, d - 1],
-            device_id=(x_to, z_to)[kind][d],
-            device_id_type=MESH,
-        )
+    def direct_copy(m, kind, back, part):
+        start, count = parts[part]
+        return pltpu.make_async_remote_copy(
+            src_ref=packs[m % 2].at[kind, back, pl.ds(start, count)],
+            dst_ref=landed[m].at[kind, back, pl.ds(start, count)],
+            send_sem=direct_send.at[m, kind, back, part],
+            recv_sem=direct_recv.at[m, kind, back, part],
+            device_id=(x_to, z_to)[kind][(1, 3)[back]],
+            device_id_type=MESH,
+        )
+
+    def onward_copy(m, kind, back):
+        return pltpu.make_async_remote_copy(
+            src_ref=landed[m].at[kind, back, pl.ds(0, through_most)],
+            dst_ref=landed[m].at[kind, back, pl.ds(most, through_most)],
+            send_sem=onward_send.at[m, kind, back],
+            recv_sem=onward_recv.at[m, kind, back],
+            device_id=(x_to, z_to)[kind][(1, 3)[back]],
+            device_id_type=MESH,
+        )
+
+    ways = [(kind, back) for back in range(2) for kind in range(2)]
 
     def last_copy(m, kind, d):
         return pltpu.make_async_remote_copy(
@@ -218,23 +260,31 @@
         for r in range(1, 8):
             drain(middle[m].at[pl.ds(0, 16)], y_recv.at[m, r - 1])
         if m == 2:
-            drain_direct(0)
-        for d in HOPS:
-            for kind in range(2):
+            for part in range(2):
+                for kind, back in ways:
+                    direct_copy(0, kind, back, part).wait_send()
+        for part in range(2):
+            for kind, back in ways:
 
                 def one(r, carry):
-                    index = table[kind * 5, (d - 1) * 32 + r]
+                    slot_in = parts[part][0] + r
+                    index = table[kind * 5, back * 32 + slot_in]
                     for half in range(2):
-                        packs[m % 2][kind, d - 1, r, half] = middle[m][index + 16 * half]
+                        packs[m % 2][kind, back, slot_in, half] = middle[m][index + 16 * half]
                     return carry
 
-                lax.fori_loop(0, slots[d], one, 0)
-                direct_copy(m, kind, d).start()
+                lax.fori_loop(0, parts[part][1], one, 0)
+                direct_copy(m, kind, back, part).start()
+
+    def relay(m):
+        for kind, back in ways:
+            direct_copy(m, kind, back, 0).wait_recv()
+            onward_copy(m, kind, back).start()
 
     def spread(m):
-        for kind in range(2):
-            for d in HOPS:
-                direct_copy(m, kind, d).wait_recv()
+        for kind, back in ways:
+            direct_copy(m, kind, back, 1).wait_recv()
+            onward_copy(m, kind, back).wait_recv()
         drain(turned[m].at[pl.ds(0, 14)], y_send.at[m])
         for d in HOPS + (0,):
             for kind in range(2):
@@ -247,7 +297,7 @@
                     stay = table[kind * 5 + 4, spot_in] > 0
                     for half in range(2):
                         here = middle[m][near + 16 * half]
-                        there = landed[m][kind, hop, rank, half]
+                        there = landed[m][kind, hop, rank % 64 + rank // 64 * most, half]
                         brick = lax.select(jnp.broadcast_to(stay, here.shape), here, there)
                         if d == 0:
                             out[m, kind, (z, x)[kind], half, k] = brick
@@ -291,10 +341,13 @@
     gather(0)
     for d in HOPS:
         turn(2, d)
+    relay(0)
     gather(1)
     spread(0)
+    relay(1)
     gather(2)
     spread(1)
+    relay(2)
     settle(0)
     spread(2)
     settle(1)
@@ -302,8 +355,11 @@
 
     for m in range(MATS):
         drain(first[m], first_send.at[m])
-        if m:
-            drain_direct(m)
+        for kind, back in ways:
+            if m:
+                for part in range(2):
+                    direct_copy(m, kind, back, part).wait_send()
+            onward_copy(m, kind, back).wait_send()
         drain(turned[m].at[pl.ds(0, 12)], last_send.at[m])
 
 
@@ -681,11 +737,13 @@
             + [pltpu.VMEM((3, 4) + tile, bf16)]
             + [pltpu.VMEM((16, 8) + brick, bf16)] * 3
             + [pltpu.VMEM((128,) + brick, bf16)] * 3
-            + [pltpu.VMEM((2, 3, max(room), 2) + brick, bf16)] * 2
-            + [pltpu.VMEM((2, 3, max(room), 2) + brick, bf16)] * 3
+            + [pltpu.VMEM((2, 2, room[0], 2) + brick, bf16)] * 2
+            + [pltpu.VMEM((2, 2, room[0] + room[1], 2) + brick, bf16)] * 3
             + [pltpu.VMEM((8, 16, columns), f32)]
             + [dma((3,)), dma((3,)), dma((3, 3)), dma((3,)), dma((3, 7))]
-            + [dma((3, 2, 3)), dma((3, 2, 3)), dma((3,)), dma((3, 2, 3))]
+            + [dma((3, 2, 2, 2))] * 2
+            + [dma((3, 2, 2))] * 2
+            + [dma((3,)), dma((3, 2, 3))]
         )
         moved, early = pl.pallas_call(
             functools.partial(direct_kernel, room),

time: 193 us -> 189 us (0.979)
  Pallas kernels: 191 us -> 187 us
    pallas_call x1, Pallas kernels: 185 us -> 180 us  [direct(): pl.pallas_call(functools.partial(direct_kernel, room), out_shape=[pltpu.V...]
where the time goes in v4:
time: 189 us
  Pallas kernels  187 us (99%)
    pallas_call x1, Pallas kernels, direct(): pl.pallas_call(functools.partial(direct_kernel, room), out_shape=[pltpu.V...  180 us
    pallas_call x1, Pallas kernels, direct(): pl.pallas_call(write_kernel, in_specs=[vmem, vmem], out_specs=[any_space,...  4.71 us

profile of v4, /device:TPU:1, one launch (start us, length us, event | category | flops | bytes accessed | tf_op | source)
XLA Modules:
  0.0 189.0 jit_solution(106096116932228444)
XLA Ops:
  0.6 2.1 %plan.1 = (s32[16,128]{1,0:T(8,128)S(1)}, s32[1]{0:T(128)}) custom-call(s32[1,128]{1,0:T(1,128)} %bitcast.3, s32[1,128]{1,0:T(1,128)} %bitcast.4), custom_call_target="tpu_custom_call" | custom-call | tf_op jit(solution)/shard_map/plan/pallas_call | solution.py:723
  3.4 185.4 %conditional.1 = ((bf16[3,1,1,8,96,2048]{5,4,3,2,1,0:T(8,128)(2,1)}, f32[3,1,1,16,768]{4,3,2,1,0:T(8,128)})) conditional(s32[]{:T(128)} %bitcast.2, (s32[16,128]{1,0:T(8,128)S(1)}, bf16[4,512,768]{2,1,0:T(8,128)(2,1)}, bf16[4,512,768]{2,1,0:T(8,128)(2,1)}, bf16[4,512,768]{2,1,0:T(8,128)(2,1)}) %tuple.19, ...), branch_computations={%region_0.0_spmd, %region_1.0_spmd, %region_2.0_spmd, %region_3.5_... | conditional | flops 54816 | bytes 3483 | solution.py:776
  3.4 180.5 %direct.3 = (bf16[3,2,4,2,8,96,128]{6,5,4,3,2,1,0:T(8,128)(2,1)S(1)}, f32[2,16,768]{2,1,0:T(8,128)S(1)}) custom-call(s32[16,128]{1,0:T(8,128)S(1)} %get-tuple-element.34.table, bf16[4,512,768]{2,1,0:T(8,128)(2,1)} %get-tuple-element.35.gate, bf16[4,512,768]{2,1,0:T(8,128)(2,1)} %get-tuple-element.36.up, bf16[4,512,768]{2,1,0:T(8,128)(2,1)} %get-tuple-element.37.down), custom_call_target="tpu_custom_call" | custom-call | tf_op jit(solution)/shard_map/cond/branch_0_fun/direct/pallas_call | solution.py:748
  183.8 4.7 %write.3 = (bf16[3,1,1,8,96,2048]{5,4,3,2,1,0:T(8,128)(2,1)}, f32[3,1,1,16,768]{4,3,2,1,0:T(8,128)}) custom-call(bf16[3,2,4,2,8,96,128]{6,5,4,3,2,1,0:T(8,128)(2,1)S(1)} %get-tuple-element.38.moved, f32[2,16,768]{2,1,0:T(8,128)S(1)} %get-tuple-element.39.early), custom_call_target="tpu_custom_call" | custom-call | tf_op jit(solution)/shard_map/cond/branch_0_fun/write/pallas_call | solution.py:759

commit v5 on v4

--- a/solution.py
+++ b/solution.py
@@ -12,7 +12,7 @@
 MESH = pl.DeviceIdType.MESH
 MATS = 3
 HOPS = (1, 3, 2)
-ROOMS = ((14, 6), (15, 7), (16, 8))
+ROOMS = ((13, 6), (14, 6), (15, 7), (16, 8))
 
 
 def device(x, z, s8):
@@ -55,49 +55,50 @@
 def plan_kernel(source_ref, target_ref, table_ref, level_ref):
     x, z, _, _ = place()
     f32, i32 = jnp.float32, jnp.int32
-    shape = (128, 128)
-    row = lax.broadcasted_iota(i32, shape, 0)
-    lane = lax.broadcasted_iota(i32, shape, 1)
-    source = jnp.broadcast_to(source_ref[...].astype(f32), shape).T
-    target = jnp.broadcast_to(target_ref[...].astype(f32), shape)
-    found = jnp.where(source == target, lane.astype(f32), 0.0)
-    to = jnp.broadcast_to(jnp.sum(found, axis=1, keepdims=True), shape).astype(i32)
-    x_to, z_to = to // 32, (to // 8) % 4
-    x_at, z_at = row // 32, (row // 8) % 4
-    inner = ((row // 4) % 2) * 32 + row % 4
-
-    def down(values):
-        return jnp.sum(values.astype(f32), axis=0, keepdims=True).astype(i32)
+    square = (128, 128)
+    row = lax.broadcasted_iota(i32, square, 0)
+    lane = lax.broadcasted_iota(i32, square, 1)
+    p = lax.broadcasted_iota(i32, (1, 128), 1)
+
+    def upright(values):
+        return jnp.broadcast_to(values.astype(f32), square).T
+
+    def total(values):
+        return jnp.sum(values, axis=0, keepdims=True).astype(i32)
+
+    wanted = upright(target_ref[...]) == source_ref[...].astype(f32)
+    to = total(jnp.where(wanted, row.astype(f32), 0.0))
+    to_row = upright(to).astype(i32)
+
+    def plane(slot, kind):
+        return slot // 32 if kind == 0 else (slot // 8) % 4
 
     kinds = []
-    misfit = [jnp.zeros(shape, f32)] * len(ROOMS)
+    worst = jnp.zeros((1, 128), i32)
     for kind in range(2):
-        at, end = (x_at, x_to) if kind == 0 else (z_at, z_to)
+        at, end = plane(p, kind), plane(to, kind)
         away = (end - at + 4) % 4
-        at_lane, away_lane = at.astype(f32).T, away.astype(f32).T
-        near = at_lane == at.astype(f32)
+        key_row = plane(row, kind) * 4 + plane(to_row, kind)
 
         def count(which):
-            return jnp.broadcast_to(
-                jnp.sum(jnp.where(which, 1.0, 0.0), axis=1, keepdims=True), shape
-            ).astype(i32)
-
-        rank = count(near & (away_lane == away.astype(f32)) & (lane < row))
-        ahead, across, behind = (count(near & (away_lane == float(d))) for d in (1, 2, 3))
+            return total(jnp.where(which, 1.0, 0.0))
+
+        rank = count((key_row == at * 4 + end) & (row < lane))
+        ahead, across, behind = (count(key_row == at * 4 + (at + d) % 4) for d in (1, 2, 3))
         kinds.append((at, away, rank, ahead, across, behind))
-        for i, (most, through_most) in enumerate(ROOMS):
+        misfit = jnp.zeros((1, 128), i32)
+        for most, through_most in ROOMS:
             low, high = window(ahead, across, behind, most, through_most)
-            misfit[i] = jnp.maximum(misfit[i], jnp.where(low > high, 1.0, 0.0))
-    level = jnp.int32(0)
-    for bad in misfit:
-        level += jnp.max(bad).astype(i32)
+            misfit += jnp.where(low > high, 1, 0)
+        worst = jnp.maximum(worst, misfit)
+    level = jnp.max(worst.astype(f32)).astype(i32)
     level_ref[0] = level
     most, through_most = jnp.int32(ROOMS[-1][0]), jnp.int32(ROOMS[-1][1])
     for i in reversed(range(len(ROOMS) - 1)):
         most = jnp.where(level <= i, ROOMS[i][0], most)
         through_most = jnp.where(level <= i, ROOMS[i][1], through_most)
 
-    table_ref[8:16, :] = jnp.zeros((8, 128), i32)
+    table_ref[...] = jnp.zeros((8, 128), i32)
     for kind in range(2):
         at, away, rank, ahead, across, behind = kinds[kind]
         low, high = window(ahead, across, behind, most, through_most)
@@ -108,24 +109,21 @@
             right + rank,
             jnp.where(away == 3, across - right + rank, jnp.where(rank < right, rank, rank - right)),
         )
-        index = kind * 64 + inner + (z_at if kind == 0 else x_at) * 4
-        mine = x if kind == 0 else z
-        sent = (at == mine) & (away > 0) & (back == lane // 32) & (slot == lane % 32)
-        step = lane // 8
-        if kind == 0:
-            place_here = (x * 4 + (z + step) % 4) * 8 + lane % 8
-        else:
-            place_here = (((x + step) % 4) * 4 + z) * 8 + lane % 8
-        got = (to == place_here) & (lane < 32)
-        moved = got & (away > 0)
-        base = kind * 5
-        table_ref[base : base + 1, :] = down(jnp.where(sent, index, 0))
-        table_ref[base + 1 : base + 2, :] = down(jnp.where(got & (away == 0), index, 0))
-        table_ref[base + 2 : base + 3, :] = down(jnp.where(moved, back, 0))
-        table_ref[base + 3 : base + 4, :] = down(
-            jnp.where(moved, slot + jnp.where(away == 2, 64, 0), 0)
-        )
-        table_ref[base + 4 : base + 5, :] = down(jnp.where(got & (away == 0), 1, 0))
+        index = kind * 64 + ((p // 4) % 2) * 32 + plane(p, 1 - kind) * 4 + p % 4
+        mine = (x, z)[kind]
+        send = jnp.where((at == mine) & (away > 0), back * 32 + slot, 127)
+        step = (plane(to, 1 - kind) - (z, x)[kind] + 4) % 4
+        receive = jnp.where(plane(to, kind) == mine, step * 8 + to % 8, 127)
+        code = jnp.where(
+            away == 0,
+            32768 + index,
+            back * 16384 + (slot + jnp.where(away == 2, 64, 0)) * 128,
+        )
+        for i, (spot, value) in enumerate(((send, index), (receive, code))):
+            joint = upright(spot * 65536 + value).astype(i32)
+            here = (joint // 65536 == lane) & (lane < 127)
+            found = total(jnp.where(here, (joint % 65536).astype(f32), 0.0))
+            table_ref[kind * 2 + i : kind * 2 + i + 1, :] = found
 
 
 def quantize(load, store, columns):
@@ -141,14 +139,13 @@
 
 def direct_kernel(room, table, gate, up, down, out, scales, *scratch):
     first = scratch[0:3]
-    own = scratch[3]
-    turned = scratch[4:7]
-    middle = scratch[7:10]
-    packs = scratch[10:12]
-    landed = scratch[12:15]
-    found = scratch[15]
-    own_sem, first_send, first_recv, y_send, y_recv = scratch[16:21]
-    direct_send, direct_recv, onward_send, onward_recv, last_send, last_recv = scratch[21:27]
+    turned = scratch[3:6]
+    middle = scratch[6:9]
+    packs = scratch[9:11]
+    landed = scratch[11:14]
+    found = scratch[14]
+    first_send, first_recv, y_send, y_recv = scratch[15:19]
+    direct_send, direct_recv, onward_send, onward_recv, last_send, last_recv = scratch[19:25]
     weights = (gate, up, down)
     most, through_most = room
     parts = ((0, through_most), (through_most, most - through_most))
@@ -176,15 +173,15 @@
     def first_copy(m, d):
         return pltpu.make_async_remote_copy(
             src_ref=rows(m, d),
-            dst_ref=first[m].at[d - 1],
+            dst_ref=first[m].at[d],
             send_sem=first_send.at[m],
-            recv_sem=first_recv.at[m, d - 1],
+            recv_sem=first_recv.at[m, d],
             device_id=tuple(pick(a, b) for a, b in zip(z_to[d], x_to[d])),
             device_id_type=MESH,
         )
 
     def own_copy(m):
-        return pltpu.make_async_copy(rows(m, 0), own.at[m], own_sem.at[m])
+        return pltpu.make_async_copy(rows(m, 0), first[m].at[0], first_recv.at[m, 0])
 
     slot = (core * 4 + yl * 2 + q // 2) * 16
 
@@ -239,22 +236,22 @@
             first_copy(m, d).start()
         own_copy(m).start()
 
-    def turn(m, d):
-        if d:
-            first_copy(m, d).wait_recv()
-            tiles = first[m].at[d - 1]
-        else:
-            own_copy(m).wait()
-            tiles = own.at[m]
-
-        def one(i, carry):
-            turned[m][origin(d) + i] = tiles[i].T.reshape(units, columns, BLOCK)
+    def turn(m, low, high):
+        def group(step, carry):
+            d = flip(step, step // 2)
+            drain(first[m].at[d], first_recv.at[m, d])
+
+            def one(i, inner):
+                turned[m][origin(d) + i] = first[m][d, i].T.reshape(units, columns, BLOCK)
+                return inner
+
+            lax.fori_loop(0, 4, one, 0)
+            for r in (2, 4, 6, 3, 5, 7, 1):
+                y_copy(m, d, r).start()
+            middle[m][pl.ds(slot + origin(d), 4)] = turned[m][pl.ds(origin(d), 4), s8]
             return carry
 
-        lax.fori_loop(0, 4, one, 0)
-        for r in (2, 4, 6, 3, 5, 7, 1):
-            y_copy(m, d, r).start()
-        middle[m][pl.ds(slot + origin(d), 4)] = turned[m][pl.ds(origin(d), 4), s8]
+        lax.fori_loop(low, high, group, 0)
 
     def gather(m):
         for r in range(1, 8):
@@ -268,7 +265,7 @@
 
                 def one(r, carry):
                     slot_in = parts[part][0] + r
-                    index = table[kind * 5, back * 32 + slot_in]
+                    index = table[kind * 2, back * 32 + slot_in]
                     for half in range(2):
                         packs[m % 2][kind, back, slot_in, half] = middle[m][index + 16 * half]
                     return carry
@@ -290,11 +287,11 @@
             for kind in range(2):
 
                 def one(k, carry):
-                    spot_in = d * 8 + k
-                    near = table[kind * 5 + 1, spot_in]
-                    hop = table[kind * 5 + 2, spot_in]
-                    rank = table[kind * 5 + 3, spot_in]
-                    stay = table[kind * 5 + 4, spot_in] > 0
+                    code = table[kind * 2 + 1, d * 8 + k]
+                    near = code % 128
+                    hop = code // 16384 % 2
+                    rank = code // 128 % 128
+                    stay = code // 32768 > 0
                     for half in range(2):
                         here = middle[m][near + 16 * half]
                         there = landed[m][kind, hop, rank % 64 + rank // 64 * most, half]
@@ -331,16 +328,13 @@
 
     for m in range(MATS):
         start(m)
-    turn(0, 0)
-    turn(1, 0)
-    for d in HOPS:
-        turn(0, d)
-    for d in HOPS:
-        turn(1, d)
-    turn(2, 0)
+    turn(0, 0, 1)
+    turn(1, 0, 1)
+    turn(0, 1, 4)
+    turn(1, 1, 4)
+    turn(2, 0, 1)
     gather(0)
-    for d in HOPS:
-        turn(2, d)
+    turn(2, 1, 4)
     relay(0)
     gather(1)
     spread(0)
@@ -354,7 +348,7 @@
     settle(2)
 
     for m in range(MATS):
-        drain(first[m], first_send.at[m])
+        drain(first[m].at[pl.ds(1, 3)], first_send.at[m])
         for kind, back in ways:
             if m:
                 for part in range(2):
@@ -511,7 +505,8 @@
         )
 
     def place_of(d1, d2):
-        return pick(x_from[d2] * 4 + z_from[d1], x_from[d1] * 4 + z_from[d2])
+        x_back, z_back = pick(d2, d1), pick(d1, d2)
+        return (x + 4 - x_back) % 4 * 4 + (z + 4 - z_back) % 4
 
     def turn_and_cross(m):
         own_copy(m).wait()
@@ -520,12 +515,21 @@
             turned[m][place] = tile.T.reshape(units, columns, BLOCK)
 
         turn(own[m], place_of(0, 0))
-        for d1 in HOPS:
-            turn(first[m][d1 - 1, tile2[0]], place_of(d1, 0))
+
+        def near(i, carry):
+            turn(first[m][i, tile2[0]], place_of(i + 1, 0))
+            return carry
+
+        lax.fori_loop(0, 3, near, 0)
         for d1 in (0,) + HOPS:
             for d2 in HOPS:
                 second_copy(m, d1, d2).wait_recv()
-                turn(second[m][d2 - 1, d1], place_of(d1, d2))
+
+        def far(i, carry):
+            turn(second[m][i // 4, i % 4], place_of(i % 4, i // 4 + 1))
+            return carry
+
+        lax.fori_loop(0, 12, far, 0)
         for r in range(1, 8):
             y_copy(m, r).start()
         middle[m][pl.ds(s8 * 16, 16)] = turned[m][:, s8]
@@ -723,7 +727,7 @@
     table, level = pl.pallas_call(
         plan_kernel,
         out_shape=[
-            jax.ShapeDtypeStruct((16, 128), jnp.int32),
+            jax.ShapeDtypeStruct((8, 128), jnp.int32),
             jax.ShapeDtypeStruct((1,), jnp.int32),
         ],
         in_specs=[vmem, vmem],
@@ -733,14 +737,13 @@
 
     def direct(room, number, table, gate, up, down, source_order, target_order):
         scratch = (
-            [pltpu.VMEM((3, 4) + tile, bf16)] * 3
-            + [pltpu.VMEM((3, 4) + tile, bf16)]
+            [pltpu.VMEM((4, 4) + tile, bf16)] * 3
             + [pltpu.VMEM((16, 8) + brick, bf16)] * 3
             + [pltpu.VMEM((128,) + brick, bf16)] * 3
             + [pltpu.VMEM((2, 2, room[0], 2) + brick, bf16)] * 2
             + [pltpu.VMEM((2, 2, room[0] + room[1], 2) + brick, bf16)] * 3
             + [pltpu.VMEM((8, 16, columns), f32)]
-            + [dma((3,)), dma((3,)), dma((3, 3)), dma((3,)), dma((3, 7))]
+            + [dma((3,)), dma((3, 4)), dma((3,)), dma((3, 7))]
             + [dma((3, 2, 2, 2))] * 2
             + [dma((3, 2, 2))] * 2
             + [dma((3,)), dma((3, 2, 3))]

time: 189 us -> 189 us (level)
  no operation moved by 1% of the time
where the time goes in v5:
time: 189 us
  Pallas kernels  187 us (99%)
    pallas_call x1, Pallas kernels, direct(): pl.pallas_call(functools.partial(direct_kernel, room), out_shape=[pltpu.V...  181 us
    pallas_call x1, Pallas kernels, direct(): pl.pallas_call(write_kernel, in_specs=[vmem, vmem], out_specs=[any_space,...  4.71 us

profile of v5, /device:TPU:1, one launch (start us, length us, event | category | flops | bytes accessed | tf_op | source)
XLA Modules:
  0.0 188.7 jit_solution(928548706313211426)
XLA Ops:
  0.6 1.7 plan.1
  3.0 185.6 %conditional.1 = ((bf16[3,1,1,8,96,2048]{5,4,3,2,1,0:T(8,128)(2,1)}, f32[3,1,1,16,768]{4,3,2,1,0:T(8,128)})) conditional(s32[]{:T(128)} %bitcast.2, (s32[8,128]{1,0:T(8,128)S(1)}, bf16[4,512,768]{2,1,0:T(8,128)(2,1)}, bf16[4,512,768]{2,1,0:T(8,128)(2,1)}, bf16[4,512,768]{2,1,0:T(8,128)(2,1)}) %tuple.22, ...), branch_computations={%region_0.0_spmd, %region_1.0_spmd, %region_2.0_spmd, %region_3.0_... | conditional | flops 54816 | bytes 3483 | solution.py:779
  3.0 180.6 %direct.5 = (bf16[3,2,4,2,8,96,128]{6,5,4,3,2,1,0:T(8,128)(2,1)S(1)}, f32[2,16,768]{2,1,0:T(8,128)S(1)}) custom-call(s32[8,128]{1,0:T(8,128)S(1)} %get-tuple-element.48.table, bf16[4,512,768]{2,1,0:T(8,128)(2,1)} %get-tuple-element.49.gate, bf16[4,512,768]{2,1,0:T(8,128)(2,1)} %get-tuple-element.50.up, bf16[4,512,768]{2,1,0:T(8,128)(2,1)} %get-tuple-element.51.down), custom_call_target="tpu_custom_call" | custom-call | tf_op jit(solution)/shard_map/cond/branch_1_fun/direct/pallas_call | solution.py:751
  183.6 4.7 %write.5 = (bf16[3,1,1,8,96,2048]{5,4,3,2,1,0:T(8,128)(2,1)}, f32[3,1,1,16,768]{4,3,2,1,0:T(8,128)}) custom-call(bf16[3,2,4,2,8,96,128]{6,5,4,3,2,1,0:T(8,128)(2,1)S(1)} %get-tuple-element.52.moved, f32[2,16,768]{2,1,0:T(8,128)S(1)} %get-tuple-element.53.early), custom_call_target="tpu_custom_call" | custom-call | tf_op jit(solution)/shard_map/cond/branch_1_fun/write/pallas_call | solution.py:762
